TPU v7x, 32 devices: a 4x4x1 block of a 4x4x8 slice. The times are simulated.
32 devices in a mesh: rep: 2 (over z, core), dp: 16 (over x, y).
Axes of the slice: x: 4, y: 4, z: 1, core: 2. Of those that a mesh axis runs over, the one named last changes fastest.
The devices are a block of a 4x4x8 slice.
Arguments:
- x: bfloat16 [32, 4096, 640], P(('rep', 'dp')), parts along dimension 0
- dy: bfloat16 [32, 4096, 640], P(('rep', 'dp')), parts along dimension 0
- w_gate: bfloat16 [2, 640, 3200], P(None, 'dp')
- w_up: bfloat16 [2, 640, 3200], P(None, 'dp')
- w_down: bfloat16 [2, 3200, 640], P(None, 'dp')
- m_w_gate: float32 [2, 640, 3200], P(None, 'dp')
- m_w_up: float32 [2, 640, 3200], P(None, 'dp')
- m_w_down: float32 [2, 3200, 640], P(None, 'dp')
- v_w_gate: float32 [2, 640, 3200], P(None, 'dp')
- v_w_up: float32 [2, 640, 3200], P(None, 'dp')
- v_w_down: float32 [2, 3200, 640], P(None, 'dp')
Outputs:
- output 1: bfloat16 [4, 640, 3200], P('rep', 'dp'), parts along dimension 0
- output 2: bfloat16 [4, 640, 3200], P('rep', 'dp'), parts along dimension 0
- output 3: bfloat16 [4, 3200, 640], P('rep', 'dp'), parts along dimension 0
- output 4: float32 [4, 640, 3200], P('rep', 'dp'), parts along dimension 0
- output 5: float32 [4, 640, 3200], P('rep', 'dp'), parts along dimension 0
- output 6: float32 [4, 3200, 640], P('rep', 'dp'), parts along dimension 0
- output 7: float32 [4, 640, 3200], P('rep', 'dp'), parts along dimension 0
- output 8: float32 [4, 640, 3200], P('rep', 'dp'), parts along dimension 0
- output 9: float32 [4, 3200, 640], P('rep', 'dp'), parts along dimension 0
There are 2 independent parts. A program takes and returns all parts, laid end to end along the dimension named above; an argument that names none is the same for every part.
All inputs are finite; a program needn't handle non-finite values.
Results may differ from a plain program's by a relative error of at most 0.022.
Values are sent between devices in bfloat16 or wider.
A program may use at most 768 MiB of HBM per device.

v0:
```python
import jax
import jax.numpy as jnp
from jax import lax
from jax.sharding import PartitionSpec as P

NAMES = ("w_gate", "w_up", "w_down")


def matmul(a, w):
    return jnp.dot(a, w, preferred_element_type=jnp.float32).astype(jnp.bfloat16)


def normed(h):
    wide = h.astype(jnp.float32)
    scale = lax.rsqrt(jnp.mean(wide**2, -1, keepdims=True) + 1e-6)
    return (wide * scale).astype(jnp.bfloat16)


def layer(h, w):
    a = normed(h)
    gate = jnp.dot(a, w["w_gate"], preferred_element_type=jnp.float32)
    up = jnp.dot(a, w["w_up"], preferred_element_type=jnp.float32)
    return h + matmul((jax.nn.silu(gate) * up).astype(jnp.bfloat16), w["w_down"])


def adamw(w, m, v, g):
    m = 0.9 * m + 0.1 * g
    v = 0.95 * v + 0.05 * g * g
    step = m * lax.rsqrt(v + 1e-8) + 0.1 * w
    return (w - 0.02 * step).astype(jnp.bfloat16), m, v


def clipped(gradients, sum_of_squares, count):
    factor = jnp.minimum(1.0, 0.5 * lax.rsqrt(sum_of_squares / count + 1e-30))
    return [g * factor for g in gradients]


def solution(mesh):
    def fetched(weights, number):
        return {name: lax.all_gather(w[number], "dp", axis=0, tiled=True) for name, w in zip(NAMES, weights, strict=True)}

    def step(x, dy, *arrays):
        weights, m, v = (arrays[i : i + 3] for i in (0, 3, 6))
        layers = weights[0].shape[0]
        h, kept = x[0], []
        for number in range(layers):
            kept.append(h)
            h = layer(h, fetched(weights, number))
        by_h, mine = dy[0], [None] * layers
        for number in reversed(range(layers)):
            _, back = jax.vjp(lambda w, h: layer(h, w), fetched(weights, number), kept[number])
            by_w, by_h = back(by_h)
            mine[number] = [lax.psum_scatter(by_w[name], "dp", scatter_dimension=0, tiled=True) for name in NAMES]
        gradients = [jnp.stack([mine[number][i] for number in range(layers)]).astype(jnp.float32) for i in range(3)]
        squares = lax.psum(sum(jnp.sum(g * g) for g in gradients), "dp")
        gradients = clipped(gradients, squares, lax.psum(1, "dp") * sum(g.size for g in gradients))
        new = [adamw(w.astype(jnp.float32), m, v, g) for w, m, v, g in zip(weights, m, v, gradients, strict=True)]
        return tuple(one[which] for which in range(3) for one in new)

    states, cut = P(("rep", "dp"), None, None), P(None, "dp", None)
    return jax.shard_map(
        step,
        mesh=mesh,
        in_specs=(states, states) + (cut,) * 9,
        out_specs=(P("rep", "dp", None),) * 9,
        check_vma=False,
    )
```

profile of v0, /device:TPU:96, one launch (start us, length us, event | category | flops | bytes accessed | tf_op | source)
XLA Modules:
  0.0 992.6 jit_solution(14079947825285387559)
XLA Ops:
  7.2 0.1 all-gather.13.cloned.1.call-start
  7.3 1.9 fusion.91
  9.1 0.1 all-gather.13.cloned.1.call-update
  9.2 0.1 all-gather.15.cloned.1.call-start
  9.3 1.9 fusion.90
  11.2 0.1 all-gather.15.cloned.1.call-update
  11.2 0.1 all-gather.17.cloned.1.call-start
  11.3 1.9 fusion.89
  13.2 0.1 all-gather.17.cloned.1.call-update
  13.3 0.1 all-gather.21.cloned.1.call-start
  13.3 0.6 all-gather.21.cloned.1.call-update
  13.9 0.1 all-gather.23.cloned.1.call-start
  14.0 0.6 all-gather.23.cloned.1.call-update
  14.6 0.1 all-gather.19.cloned.1.call-start
  14.6 0.6 all-gather.19.cloned.1.call-update
  15.2 0.1 reduce-scatter.7.cloned.1.call-start
  15.3 8.0 copy.22
  23.3 3.6 fusion.15
  26.9 0.0 copy-start.10
  26.9 8.0 copy.23
  34.9 24.1 %all-gather.13.cloned.1.call-done = bf16[1,640,3200]{2,1,0:T(8,128)(2,1)} async-done(((bf16[1,40,3200]{2,1,0:T(8,128)(2,1)}), bf16[1,640,3200]{2,1,0:T(8,128)(2,1)}) %all-gather.13.cloned.1.call-update) | async-done | bytes 4096016 | tf_op jit(solution)/shard_map/all_gather | solution.py:40
  58.9 29.3 %fusion.46 = f32[4096,3200]{1,0:T(8,128)} fusion(bf16[1,640,3200]{2,1,0:T(8,128)(2,1)} %all-gather.13.cloned.1.call-done, bf16[1,4096,640]{1,2,0:T(8,128)(2,1)} %copy.22, f32[4096]{0:T(1024)S(1)} %add_rsqrt_fusion), kind=kOutput, calls=%fused_computation.65 | convolution fusion | flops 16785080320 | bytes 61784064 | tf_op jit(solution)/shard_map/dot_general | solution.py:21
  88.2 18.5 %all-gather.15.cloned.1.call-done = bf16[1,640,3200]{2,1,0:T(8,128)(2,1)} async-done(((bf16[1,40,3200]{2,1,0:T(8,128)(2,1)}), bf16[1,640,3200]{2,1,0:T(8,128)(2,1)}) %all-gather.15.cloned.1.call-update) | async-done | bytes 4096016 | tf_op jit(solution)/shard_map/all_gather | solution.py:40
  106.7 51.1 %multiply_convert_fusion.1 = (bf16[4096,3200]{1,0:T(8,128)(2,1)}, f32[4096,3200]{1,0:T(8,128)}) fusion(f32[4096,3200]{1,0:T(8,128)} %fusion.46, bf16[1,640,3200]{2,1,0:T(8,128)(2,1)} %all-gather.15.cloned.1.call-done, bf16[1,4096,640]{1,2,0:T(8,128)(2,1)} %copy.22, f32[4096]{0:T(1024)S(1)} %add_rsqrt_fusion), kind=kOutput, calls=%fused_computation.17 | convolution fusion | flops 16863723520 | bytes 140427264 | tf_op jit(solution)/shard_map/dot_general | solution.py:22
  157.8 24.8 %fusion.19 = (f32[4096]{0:T(1024)S(1)}, bf16[4096,640]{0,1:T(8,128)(2,1)}) fusion(bf16[4096,3200]{1,0:T(8,128)(2,1)} %get-tuple-element.28, bf16[1,3200,640]{2,1,0:T(8,128)(2,1)} %all-gather.17.cloned.1.call-done, bf16[1,4096,640]{1,2,0:T(8,128)(2,1)} %copy.22), kind=kOutput, calls=%fused_computation.37 | convolution fusion | flops 16790319104 | bytes 40812544 | tf_op jit(solution)/shard_map/dot_general | solution.py:10
  182.6 0.6 copy-done.8
  183.2 0.0 copy-start.6
  183.2 18.8 %all-gather.21.cloned.1.call-done = bf16[1,3200,640]{2,1,0:T(8,128)(2,1)} async-done(((bf16[1,200,640]{2,1,0:T(8,128)(2,1)}), bf16[1,3200,640]{2,1,0:T(8,128)(2,1)}) %all-gather.21.cloned.1.call-update) | async-done | bytes 4096016 | tf_op jit(solution)/shard_map/all_gather | solution.py:40
  202.0 28.1 %convolution_convert_fusion.1 = bf16[4096,3200]{1,0:T(8,128)(2,1)} fusion(bf16[1,4096,640]{2,1,0:T(8,128)(2,1)} %param.12, bf16[1,3200,640]{2,1,0:T(8,128)(2,1)} %all-gather.21.cloned.1.call-done), kind=kOutput, calls=%fused_computation.23 | convolution fusion | flops 16790323200 | bytes 35553280 | tf_op jit(solution)/shard_map/transpose(jvp())/dot_general | solution.py:10
  230.2 19.5 %all-gather.23.cloned.1.call-done = bf16[1,640,3200]{2,1,0:T(8,128)(2,1)} async-done(((bf16[1,40,3200]{2,1,0:T(8,128)(2,1)}), bf16[1,640,3200]{2,1,0:T(8,128)(2,1)}) %all-gather.23.cloned.1.call-update) | async-done | bytes 4096016 | tf_op jit(solution)/shard_map/all_gather | solution.py:40
  249.6 29.4 %fusion.35 = f32[4096,3200]{1,0:T(8,128)} fusion(bf16[1,640,3200]{2,1,0:T(8,128)(2,1)} %all-gather.23.cloned.1.call-done, bf16[4096,640]{0,1:T(8,128)(2,1)} %get-tuple-element.31, f32[4096]{0:T(1024)S(1)} %fusion.77), kind=kOutput, calls=%fused_computation.54 | convolution fusion | flops 16785080320 | bytes 61784064 | tf_op jit(solution)/shard_map/jvp()/dot_general | solution.py:22
  279.0 18.2 %all-gather.19.cloned.1.call-done = bf16[1,640,3200]{2,1,0:T(8,128)(2,1)} async-done(((bf16[1,40,3200]{2,1,0:T(8,128)(2,1)}), bf16[1,640,3200]{2,1,0:T(8,128)(2,1)}) %all-gather.19.cloned.1.call-update) | async-done | bytes 4096016 | tf_op jit(solution)/shard_map/all_gather | solution.py:40
  297.3 67.7 %fusion.2 = (bf16[4096,3200]{1,0:T(8,128)(2,1)}, f32[4096,3200]{1,0:T(8,128)}) fusion(f32[4096,3200]{1,0:T(8,128)} %fusion.35, bf16[4096,3200]{1,0:T(8,128)(2,1)} %convolution_convert_fusion.1, bf16[1,640,3200]{2,1,0:T(8,128)(2,1)} %all-gather.19.cloned.1.call-done, bf16[4096,640]{0,1:T(8,128)(2,1)} %get-tuple-element.31, f32[4096]{0:T(1024)S(1)} %fusion.77), kind=kOutput, calls=%fused_computation.8 | convolution fusion | flops 16942366720 | bytes 166641664 | tf_op jit(solution)/shard_map/jvp()/dot_general | solution.py:21
  364.9 39.8 %fusion.23 = bf16[3200,640]{1,0:T(8,128)(2,1)} fusion(f32[4096,3200]{1,0:T(8,128)} %fusion.35, bf16[1,4096,640]{2,1,0:T(8,128)(2,1)} %param.12, f32[4096,3200]{1,0:T(8,128)} %get-tuple-element.33), kind=kOutput, calls=%fused_computation.40 | convolution fusion | flops 16857907200 | bytes 114196480 | tf_op jit(solution)/shard_map/transpose(jvp())/dot_general | solution.py:10
  404.8 26.3 %convolution_convert_fusion.3 = bf16[640,3200]{1,0:T(8,128)(2,1)} fusion(bf16[4096,3200]{1,0:T(8,128)(2,1)} %get-tuple-element.32, bf16[4096,640]{0,1:T(8,128)(2,1)} %get-tuple-element.31, f32[4096]{0:T(1024)S(1)} %fusion.77), kind=kOutput, calls=%fused_computation.46 | convolution fusion | flops 16785080320 | bytes 35569664 | tf_op jit(solution)/shard_map/transpose(jvp())/dot_general | solution.py:21
  431.1 22.4 %convolution_convert_fusion.4 = bf16[4096,640]{0,1:T(8,128)(2,1)} fusion(bf16[4096,3200]{1,0:T(8,128)(2,1)} %get-tuple-element.32, bf16[1,640,3200]{2,1,0:T(8,128)(2,1)S(1)} %copy-done.12), kind=kOutput, calls=%fused_computation.47 | convolution fusion | flops 16777216000 | bytes 35553280 | tf_op jit(solution)/shard_map/transpose(jvp())/dot_general | solution.py:21
  453.5 40.6 %fusion.21 = (f32[4096]{0:T(1024)S(1)}, bf16[4096,640]{0,1:T(8,128)(2,1)}) fusion(bf16[4096,640]{0,1:T(8,128)(2,1)} %get-tuple-element.31, bf16[4096,640]{0,1:T(8,128)(2,1)} %convolution_convert_fusion.4, bf16[1,640,3200]{2,1,0:T(8,128)(2,1)} %all-gather.23.cloned.1.call-done, bf16[4096,3200]{1,0:T(8,128)(2,1)} %convolution_convert_fusion.1, ...), kind=kOutput, calls=%fused_computation.39 | convolution fusion | flops 16871583744 | bytes 98484224 | tf_op jit(solution)/shard_map/transpose(jvp())/dot_general | solution.py:22
  494.1 11.8 %fusion.32 = bf16[4096,640]{0,1:T(8,128)(2,1)} fusion(bf16[4096,640]{0,1:T(8,128)(2,1)} %get-tuple-element.31, bf16[4096,640]{0,1:T(8,128)(2,1)} %get-tuple-element.35, bf16[1,4096,640]{1,2,0:T(8,128)(2,1)} %copy.23, f32[4096]{0:T(1024)S(1)} %multiply_multiply_fusion.3, f32[4096]{0:T(1024)S(1)} %fusion.77), kind=kLoop, calls=%fused_computation.51 | loop fusion | flops 18350080 | bytes 21004288 | tf_op jit(solution)/shard_map/transpose(jvp())/add_any | solution.py:14
  506.0 26.3 %convolution_convert_fusion.2 = bf16[3200,640]{1,0:T(8,128)(2,1)} fusion(bf16[4096,3200]{1,0:T(8,128)(2,1)} %get-tuple-element.28, bf16[4096,640]{0,1:T(8,128)(2,1)} %fusion.32), kind=kOutput, calls=%fused_computation.45 | convolution fusion | flops 16779264000 | bytes 35553280 | tf_op jit(solution)/shard_map/transpose(jvp())/dot_general | solution.py:10
  532.3 0.1 reduce-scatter.7.cloned.1.call-update
  532.4 0.1 reduce-scatter.9.cloned.1.call-start
  532.4 27.4 %convolution_convert_fusion = bf16[4096,3200]{1,0:T(8,128)(2,1)} fusion(bf16[4096,640]{0,1:T(8,128)(2,1)} %fusion.32, bf16[1,3200,640]{2,1,0:T(8,128)(2,1)} %all-gather.17.cloned.1.call-done), kind=kOutput, calls=%fused_computation.22 | convolution fusion | flops 16790323200 | bytes 35553280 | tf_op jit(solution)/shard_map/transpose(jvp())/dot_general | solution.py:10
  559.8 46.6 %fusion.26 = bf16[640,3200]{1,0:T(8,128)(2,1)} fusion(f32[4096,3200]{1,0:T(8,128)} %fusion.46, f32[4096,3200]{1,0:T(8,128)} %get-tuple-element.29, bf16[4096,3200]{1,0:T(8,128)(2,1)} %convolution_convert_fusion, bf16[1,4096,640]{1,2,0:T(8,128)(2,1)} %copy.22, f32[4096]{0:T(1024)S(1)} %copy-done.11), kind=kOutput, calls=%fused_computation.43 | convolution fusion | flops 16931307520 | bytes 140427264 | tf_op jit(solution)/shard_map/transpose(jvp())/dot_general | solution.py:21
  606.5 33.2 %fusion.29 = bf16[640,3200]{1,0:T(8,128)(2,1)} fusion(bf16[4096,3200]{1,0:T(8,128)(2,1)} %convolution_convert_fusion, f32[4096,3200]{1,0:T(8,128)} %fusion.46, bf16[1,4096,640]{1,2,0:T(8,128)(2,1)S(1)} %copy-done, f32[4096]{0:T(1024)S(1)} %copy-done.11), kind=kOutput, calls=%fused_computation.44 | convolution fusion | flops 16865771520 | bytes 87998464 | tf_op jit(solution)/shard_map/transpose(jvp())/dot_general | solution.py:22
  639.7 0.1 reduce-scatter.9.cloned.1.call-update
  639.8 0.1 all-reduce.9.cloned.1.call-start
  639.8 34.5 %fusion.25 = bf16[640,3200]{1,0:T(8,128)(2,1)} fusion(bf16[4096,3200]{1,0:T(8,128)(2,1)} %convolution_convert_fusion.1, bf16[4096,640]{0,1:T(8,128)(2,1)} %get-tuple-element.31, f32[4096]{0:T(1024)S(1)} %copy-done.7, f32[4096,3200]{1,0:T(8,128)} %get-tuple-element.33), kind=kOutput, calls=%fused_computation.42 | convolution fusion | flops 16865771520 | bytes 87998464 | tf_op jit(solution)/shard_map/transpose(jvp())/dot_general | solution.py:22
  674.3 0.1 all-reduce.9.cloned.1.call-update
  674.4 0.6 copy-done.13
  675.0 0.6 dynamic-slice
  676.2 0.0 reduce-scatter.7.cloned.1.call-done
  676.3 45.0 %reduce-scatter.9.cloned.1.call-done = bf16[200,640]{1,0:T(8,128)(2,1)} async-done(((bf16[3200,640]{1,0:T(8,128)(2,1)}), bf16[200,640]{1,0:T(8,128)(2,1)}) %reduce-scatter.9.cloned.1.call-update) | async-done | bytes 256016
  721.2 1.9 fusion.67
  723.2 207.5 %all-reduce.9.cloned.1.call-done = (bf16[640,3200]{1,0:T(8,128)(2,1)}, bf16[640,3200]{1,0:T(8,128)(2,1)}, bf16[640,3200]{1,0:T(8,128)(2,1)}, bf16[640,3200]{1,0:T(8,128)(2,1)}) async-done(((bf16[640,3200]{1,0:T(8,128)(2,1)}, bf16[640,3200]{1,0:T(8,128)(2,1)}, bf16[640,3200]{1,0:T(8,128)(2,1)}, bf16[640,3200]{1,0:T(8,128)(2,1)}), (bf16[640,3200]{1,0:T(8,128)(2,1)}, bf16[640,3200]{1,0:T(8,128)(2,1)}, ...) | async-done | bytes 16384016
  930.7 1.1 dynamic-slice_bitcast_fusion
  931.8 0.9 fusion.66
  932.6 1.1 dynamic-slice_bitcast_fusion.2
  933.7 0.9 fusion.65
  936.5 39.7 %psum.7 = f32[]{:T(128)} all-reduce(f32[]{:T(128)S(6)} %add.99), channel_id=1, replica_groups=mesh['rep'=2,'dp'=16] {'dp'}, use_global_device_ids=true, to_apply=%region_12.13 | all-reduce | flops 1 | bytes 8 | tf_op jit(solution)/shard_map/psum | solution.py:55
  976.9 0.0 copy-start.4
  976.9 0.0 copy-start.5
  976.9 3.6 fusion.73
  980.6 3.3 fusion.70
  983.9 1.7 fusion.64
  (26 shorter events, 0.1 us)
Async XLA Ops:
  7.2 51.7 %all-gather.13.cloned.1.call-start = ((), (), s32[]{:S(2)}) async-start(), calls=%async_computation.2 | async-start | bytes 4352000 | tf_op jit(solution)/shard_map/all_gather | solution.py:40
  9.2 97.5 %all-gather.15.cloned.1.call-start = ((), (), s32[]{:S(2)}) async-start(), calls=%async_computation.3 | async-start | bytes 4352000 | tf_op jit(solution)/shard_map/all_gather | solution.py:40
  11.2 146.6 %all-gather.17.cloned.1.call-start = ((), (), s32[]{:S(2)}) async-start(), calls=%async_computation.4 | async-start | bytes 4352000 | tf_op jit(solution)/shard_map/all_gather | solution.py:40
  13.3 188.8 %all-gather.21.cloned.1.call-start = ((), (), s32[]{:S(2)}) async-start(), calls=%async_computation.6 | async-start | bytes 4352000 | tf_op jit(solution)/shard_map/all_gather | solution.py:40
  13.9 235.7 %all-gather.23.cloned.1.call-start = ((), (), s32[]{:S(2)}) async-start(), calls=%async_computation.7 | async-start | bytes 4352000 | tf_op jit(solution)/shard_map/all_gather | solution.py:40
  14.6 282.7 %all-gather.19.cloned.1.call-start = ((), (), s32[]{:S(2)}) async-start(), calls=%async_computation.5 | async-start | bytes 4352000 | tf_op jit(solution)/shard_map/all_gather | solution.py:40
  15.2 661.1 %reduce-scatter.7.cloned.1.call-start = ((), (), s32[]{:S(2)}) async-start(), calls=%async_computation.8 | async-start | bytes 4352000
  26.9 79.8 %copy-start.10 = (f32[4096]{0:T(1024)}, f32[4096]{0:T(1024)S(1)}, u32[]{:S(2)}) copy-start(f32[4096]{0:T(1024)S(1)} %add_rsqrt_fusion) | copy-start | bytes 49156
  182.6 0.6 copy-start.8
  183.2 310.9 %copy-start.6 = (f32[4096]{0:T(1024)}, f32[4096]{0:T(1024)S(1)}, u32[]{:S(2)}) copy-start(f32[4096]{0:T(1024)S(1)} %fusion.77) | copy-start | bytes 49156
  404.8 26.3 %copy-start.12 = (bf16[1,640,3200]{2,1,0:T(8,128)(2,1)S(1)}, bf16[1,640,3200]{2,1,0:T(8,128)(2,1)}, u32[]{:S(2)}) copy-start(bf16[1,640,3200]{2,1,0:T(8,128)(2,1)} %all-gather.19.cloned.1.call-done) | copy-start | bytes 12288004
  453.5 40.6 %copy-start.9 = (f32[4096]{0:T(1024)S(1)}, f32[4096]{0:T(1024)}, u32[]{:S(2)}) copy-start(f32[4096]{0:T(1024)} %copy-done.8) | copy-start | bytes 49156
  532.3 27.5 %copy-start.11 = (f32[4096]{0:T(1024)S(1)}, f32[4096]{0:T(1024)}, u32[]{:S(2)}) copy-start(f32[4096]{0:T(1024)} %copy-done.10) | copy-start | bytes 49156
  532.4 188.9 %reduce-scatter.9.cloned.1.call-start = ((), (), s32[]{:S(2)}) async-start(), calls=%async_computation.9 | async-start | bytes 4352000
  559.8 46.6 %copy-start = (bf16[1,4096,640]{1,2,0:T(8,128)(2,1)S(1)}, bf16[1,4096,640]{1,2,0:T(8,128)(2,1)}, u32[]{:S(2)}) copy-start(bf16[1,4096,640]{1,2,0:T(8,128)(2,1)} %copy.22) | copy-start | bytes 15728644
  606.5 33.4 %copy-start.7 = (f32[4096]{0:T(1024)S(1)}, f32[4096]{0:T(1024)}, u32[]{:S(2)}) copy-start(f32[4096]{0:T(1024)} %copy-done.6) | copy-start | bytes 49156
  639.8 290.9 %all-reduce.9.cloned.1.call-start = ((), (), s32[]{:S(2)}) async-start(), calls=%async_computation.10 | async-start | bytes 32768000
  674.3 0.7 copy-start.13
  674.3 302.6 %copy-start.1 = (bf16[2,200,640]{2,1,0:T(8,128)(2,1)S(1)}, bf16[2,200,640]{2,1,0:T(8,128)(2,1)}, u32[]{:S(2)}) copy-start(bf16[2,200,640]{2,1,0:T(8,128)(2,1)} %param.15) | copy-start | bytes 1536004
  674.3 306.2 %copy-start.2 = (bf16[2,40,3200]{2,1,0:T(8,128)(2,1)S(1)}, bf16[2,40,3200]{2,1,0:T(8,128)(2,1)}, u32[]{:S(2)}) copy-start(bf16[2,40,3200]{2,1,0:T(8,128)(2,1)} %param.14) | copy-start | bytes 1536004
  674.4 309.4 %copy-start.3 = (bf16[2,40,3200]{2,1,0:T(8,128)(2,1)S(1)}, bf16[2,40,3200]{2,1,0:T(8,128)(2,1)}, u32[]{:S(2)}) copy-start(bf16[2,40,3200]{2,1,0:T(8,128)(2,1)} %param.13) | copy-start | bytes 1536004
  976.9 6.9 copy-start.4
  976.9 6.9 copy-start.5
Sparse Core Ops, SparseCore 0:
  10.6 48.2 all-gather.12
  61.5 45.1 all-gather.14
  109.3 45.1 all-gather.16
  156.9 45.1 all-gather.20
  204.5 45.1 all-gather.22
  252.1 45.1 all-gather.18
  532.5 81.3 reduce-scatter.6
  639.9 81.3 reduce-scatter.8
  725.5 205.0 all-reduce.8
where the time goes:
time: 1000 us; the launch traced here: 993 us
  matrix products  528 us (53%)
  waiting for transfers between devices  354 us (35%)
  blocking collectives  39.7 us (4%)
  other arithmetic  27.8 us (3%)
  local copies, waits for them, and re-layouts  25.7 us (3%)
  between operations  17.7 us (2%)
    unnamed x12, waiting for transfers between devices  254 us
    dot_general x5, matrix products, layer(): gate = jnp.dot(a, w['w_gate'], preferred_element_type=jnp.float32)  192 us
    dot_general x5, matrix products, layer(): up = jnp.dot(a, w['w_up'], preferred_element_type=jnp.float32)  189 us
    dot_general x5, matrix products, matmul(): jnp.dot(a, w, preferred_element_type=jnp.float32).astype(jnp.bfloat16)  146 us
    all_gather x6, waiting for transfers between devices, fetched(): lax.all_gather(w[number], 'dp', axis=0, tiled=True)  99 us
    psum x1, blocking collectives, step(): squares = lax.psum(sum((jnp.sum(g * g) for g in gradients)), 'dp')  39.7 us
  transfers between devices with their start and end apart: 9, of which 7 were waited for; matrix products, arithmetic and copies ran while one was open for 33% of the time, Pallas kernels for 0%

commit v1 on v0

v1 whole, which is shorter than its diff:
```python
import functools
import math

import jax
import jax.numpy as jnp
from jax import lax
from jax.experimental import pallas as pl
from jax.experimental.pallas import tpu as pltpu
from jax.sharding import PartitionSpec as P

BF, F32 = jnp.bfloat16, jnp.float32
LANES = 128
VMEM = 67000000


def place(side):
    me = lax.axis_index("dp")
    x, y = me // side, me % side
    on, back = (x + 1) % side, (x + side - 1) % side
    up, down = (y + 1) % side, (y + side - 1) % side
    return x, y, {"x": (on * side + y, back * side + y), "y": (x * side + up, x * side + down)}


def greet(near):
    barrier = pltpu.get_barrier_semaphore()
    for pair in near.values():
        for other in pair:
            pl.semaphore_signal(barrier, inc=1, device_id={"dp": other}, device_id_type=pl.DeviceIdType.MESH)
    pl.semaphore_wait(barrier, 4)


def remote(src, dst, sems, number, to):
    return pltpu.make_async_remote_copy(
        src_ref=src, dst_ref=dst, send_sem=sems[0].at[number], recv_sem=sems[1].at[number], device_id={"dp": to}, device_id_type=pl.DeviceIdType.MESH
    )


def half(n):
    return (n // LANES + 1) // 2 * LANES


def all_gather_events(side, shards, whole, sems, local):
    x, y, near = place(side)
    cut = (shards[2].shape[0] + 1) // 2
    flows = []
    for k in range(2):
        ref = whole[k]
        flows.append(("xy"[k], shards[k], lambda i, j, ref=ref: ref.at[i, j]))
    for k, (lo, n) in enumerate(((0, cut), (cut, shards[2].shape[0] - cut))):
        flows.append(("xy"[k], shards[2].at[pl.ds(lo, n)], lambda i, j, lo=lo, n=n: whole[2].at[pl.ds(lo, n), i, j]))
    every = pl.ds(0, side)

    def copies(step):
        out = []
        for k, (first, mine, at) in enumerate(flows):
            second = "y" if first == "x" else "x"
            c1, c2 = (x, y) if first == "x" else (y, x)

            def spot(a, b, at=at, first=first):
                return at(a, b) if first == "x" else at(b, a)

            lanes = mine.shape[-1]
            cut_at = half(lanes)
            if step == 0:
                pairs = [(near[first][i], mine, spot(c1, c2)) for i in range(2)]
            elif step == 1:
                pairs = []
                for i, (lo, n) in enumerate(((0, cut_at), (cut_at, lanes - cut_at))):
                    origin = (c1 + (side - 1 if i == 0 else 1)) % side
                    ref = spot(origin, c2)
                    part = ref.at[(slice(None),) * (len(ref.shape) - 1) + (pl.ds(lo, n),)]
                    pairs.append((near[first][i], part, part))
            elif step == 2:
                pairs = [(near[second][i], spot(every, c2), spot(every, c2)) for i in range(2)]
            else:
                pairs = []
                for i in range(2):
                    origin = (c2 + (side - 1 if i == 0 else 1)) % side
                    ref = spot(pl.ds(i * (side // 2), side // 2), origin)
                    pairs.append((near[second][i], ref, ref))
            for i, (to, src, dst) in enumerate(pairs):
                out.append(remote(src, dst, sems, (k * 4 + step) * 2 + i, to))
        return out

    own = [pltpu.make_async_copy(mine, at(x, y), local.at[k]) for k, (_, mine, at) in enumerate(flows)]

    def begin():
        greet(near)
        for c in own:
            c.start()
        for c in copies(0):
            c.start()

    def middle(step):
        for c in copies(step - 1):
            c.wait_recv()
        if step == 2:
            for c in own:
                c.wait()
        for c in copies(step):
            c.start()

    def finish():
        for c in copies(3):
            c.wait_recv()
        for step in range(4):
            for c in copies(step):
                c.wait_send()

    return [begin, functools.partial(middle, 1), functools.partial(middle, 2), functools.partial(middle, 3), finish]


AG_SEMS = [pltpu.SemaphoreType.DMA((32,)), pltpu.SemaphoreType.DMA((32,)), pltpu.SemaphoreType.DMA((4,))]


def gathered_shapes(side, shards):
    up, down = shards[0], shards[2]
    wide = jax.ShapeDtypeStruct((side, side) + up.shape, BF)
    return [wide, wide, jax.ShapeDtypeStruct((down.shape[0], side, side) + down.shape[1:], BF)]


def flat(whole):
    gate, up, down = whole
    d = gate.shape[0] * gate.shape[1] * gate.shape[2]
    return gate.reshape(d, -1), up.reshape(d, -1), down.reshape(-1, down.shape[-1])


def gather_kernel(side, *refs):
    shards, whole, (send, recv, local) = refs[:3], refs[3:6], refs[6:]
    for event in all_gather_events(side, shards, whole, (send, recv), local):
        event()


def gather(side, shards):
    return pl.pallas_call(
        functools.partial(gather_kernel, side),
        out_shape=gathered_shapes(side, shards),
        in_specs=[pl.BlockSpec(memory_space=pl.ANY)] * 3,
        out_specs=[pl.BlockSpec(memory_space=pl.ANY)] * 3,
        scratch_shapes=AG_SEMS,
        compiler_params=pltpu.CompilerParams(collective_id=0, has_side_effects=True),
        name="gather",
    )(*shards)


def norm(h):
    wide = h.astype(F32)
    scale = lax.rsqrt(jnp.mean(wide * wide, -1, keepdims=True) + 1e-6)
    return wide, scale


def dot(a, b, dims=((1,), (0,))):
    return lax.dot_general(a, b, (dims, ((), ())), preferred_element_type=F32)


def forward_kernel(side, steps, when, *refs):
    h_ref, wg, wu, wd = refs[:4]
    shards, out_ref, whole = refs[4:7], refs[7], refs[8:11]
    acc, (send, recv, local) = refs[11], refs[12:]
    t = pl.program_id(0)
    events = all_gather_events(side, shards, whole, (send, recv), local)
    for event, at in zip(events[:-1], when):
        pl.when(t == at)(event)
    wide, scale = norm(h_ref[...])
    a = (wide * scale).astype(BF)
    d, ff = wg.shape
    for j in range(ff // d):
        cols = pl.ds(j * d, d)
        gate, up = dot(a, wg[:, cols]), dot(a, wu[:, cols])
        act = (gate * jax.nn.sigmoid(gate) * up).astype(BF)
        term = dot(act, wd[cols, :])
        if j == 0:
            acc[...] = term
        else:
            acc[...] += term
    out_ref[...] = h_ref[...] + acc[...].astype(BF)
    pl.when(t == steps - 1)(events[-1])


def forward(side, h, weights, shards):
    tokens, d = h.shape
    steps = 16
    tile = tokens // steps
    ff = weights[0].shape[1]
    any_ = pl.BlockSpec(memory_space=pl.ANY)
    resident = [pl.BlockSpec(w.shape, lambda t: (0, 0)) for w in weights]
    rows = pl.BlockSpec((tile, d), lambda t: (t, 0))
    out = pl.pallas_call(
        functools.partial(forward_kernel, side, steps, (0, 3, 5, 14)),
        grid=(steps,),
        out_shape=[jax.ShapeDtypeStruct(h.shape, BF)] + gathered_shapes(side, shards),
        in_specs=[rows] + resident + [any_] * 3,
        out_specs=[rows] + [any_] * 3,
        scratch_shapes=[pltpu.VMEM((tile, d), F32)] + AG_SEMS,
        compiler_params=pltpu.CompilerParams(collective_id=1, has_side_effects=True, vmem_limit_bytes=VMEM, dimension_semantics=("arbitrary",)),
        cost_estimate=pl.CostEstimate(flops=6 * tokens * d * ff, bytes_accessed=20 * tokens * d, transcendentals=tokens * ff),
        name="forward",
    )(h, *weights, *shards)
    return out[0], out[1:]


def scatter_events(side, terms, bufs, sems, out_ref):
    x, y, near = place(side)
    r1, r2, s2, total, t2, q1a, q1b, q2, s4 = bufs
    lanes = terms.shape[-1]
    lo = half(lanes)
    part = (pl.ds(0, lo), pl.ds(lo, lanes - lo))
    h = side // 2

    def parts(k):
        first = "y" if k != 1 else "x"
        c1, c2 = (y, x) if first == "y" else (x, y)

        def at(a, b):
            return terms.at[k, b, a] if first == "y" else terms.at[k, a, b]

        return near[first], near["x" if first == "y" else "y"], c1, c2, at

    def copies(step):
        out = []
        for k in range(3):
            first, second, c1, c2, at = parts(k)
            if step == 0:
                far = (c1 + 2) % side
                pairs = [(first[i], at(far, pl.ds(i * h, h)), r1.at[k, i]) for i in range(2)]
            elif step == 1:
                pairs = [(first[i], s2.at[k, i], r2.at[k, i]) for i in range(2)]
            elif step == 2:
                pairs = [(second[i], t2.at[k, :, part[i]], (q1a, q1b)[i].at[k]) for i in range(2)]
            else:
                pairs = [(second[i], s4.at[k, i], q2.at[k, i]) for i in range(2)]
            for i, (to, src, dst) in enumerate(pairs):
                out.append(remote(src, dst, sems, (k * 4 + step) * 2 + i, to))
        return out

    def wide(ref):
        return ref[...].astype(F32)

    def zero():
        for c in copies(0):
            c.start()

    def one():
        for c in copies(0):
            c.wait_recv()
        for k in range(3):
            _, _, c1, c2, at = parts(k)
            for i in range(2):
                dest = (c1 + (1 if i == 0 else side - 1)) % side
                for b in range(side):
                    mine = at(dest, b)
                    if b // h == i:
                        s2[k, i, b] = (wide(mine) + wide(r1.at[k, i, b - i * h])).astype(BF)
                    else:
                        s2[k, i, b] = mine[...]
        for c in copies(1):
            c.start()

    def two():
        for c in copies(1):
            c.wait_recv()
        for k in range(3):
            _, _, c1, c2, at = parts(k)
            for b in range(side):
                total[k, b] = wide(at(c1, b)) + wide(r2.at[k, 0, b]) + wide(r2.at[k, 1, b])
            t2[k] = total[k, (c2 + 2) % side].astype(BF)
        for c in copies(2):
            c.start()

    def three():
        for c in copies(2):
            c.wait_recv()
        for k in range(3):
            _, _, c1, c2, at = parts(k)
            on, back = (c2 + 1) % side, (c2 + side - 1) % side
            s4[k, 0, :, part[0]] = (total[k, on, :, part[0]] + wide(q1a.at[k])).astype(BF)
            s4[k, 0, :, part[1]] = total[k, on, :, part[1]].astype(BF)
            s4[k, 1, :, part[0]] = total[k, back, :, part[0]].astype(BF)
            s4[k, 1, :, part[1]] = (total[k, back, :, part[1]] + wide(q1b.at[k])).astype(BF)
        for c in copies(3):
            c.start()

    def four(chunk):
        for c in copies(3):
            c.wait_recv()
        for k in range(3):
            _, _, c1, c2, at = parts(k)
            out_ref[chunk, k] = (total[k, c2] + wide(q2.at[k, 0]) + wide(q2.at[k, 1])).astype(BF)
        for step in range(4):
            for c in copies(step):
                c.wait_send()

    return near, (zero, one, two, three, four)


def scatter_scratch(side, rows, lanes):
    lo = half(lanes)
    return [
        pltpu.VMEM((3, 2, side // 2, rows, lanes), BF),
        pltpu.VMEM((3, 2, side, rows, lanes), BF),
        pltpu.VMEM((3, 2, side, rows, lanes), BF),
        pltpu.VMEM((3, side, rows, lanes), F32),
        pltpu.VMEM((3, rows, lanes), BF),
        pltpu.VMEM((3, rows, lo), BF),
        pltpu.VMEM((3, rows, lanes - lo), BF),
        pltpu.VMEM((3, 2, rows, lanes), BF),
        pltpu.VMEM((3, 2, rows, lanes), BF),
    ]


def backward_kernel(side, chunks, steps, when, inner, *refs):
    h_ref, by_ref, wg, wu, wd = refs[:5]
    refs = refs[5:]
    if inner:
        out_ref, by_out, refs = refs[0], refs[1], refs[2:]
        by_a, refs = refs[0], refs[1:]
    else:
        out_ref, refs = refs[0], refs[1:]
    a_s, at_s, byt_s, acc_g, acc_u, acc_d, terms = refs[:7]
    bufs, sems = refs[7:16], refs[16:18]
    j, t = pl.program_id(0), pl.program_id(1)
    tile, d = h_ref.shape
    rows = terms.shape[3]
    near, (zero, one, two, three, four) = scatter_events(side, terms, bufs, sems, out_ref)
    pl.when((j == 0) & (t == 0))(lambda: greet(near))
    later = j > 0
    pl.when(later & (t == when[0]))(zero)
    pl.when(later & (t == when[1]))(one)
    pl.when(later & (t == when[2]))(two)
    pl.when(later & (t == when[3]))(three)
    pl.when(later & (t == when[4]))(lambda: four(j - 1))

    here = pl.ds(pl.multiple_of(t * tile, tile), tile)

    @pl.when(j == 0)
    def _():
        wide, scale = norm(h_ref[...])
        a = wide * scale
        a_s[here, :] = a.astype(BF)
        at_s[t] = a.T.astype(BF)
        byt_s[t] = by_ref[...].astype(F32).T.astype(BF)

    a, by = a_s[here, :], by_ref[...]
    gate, up = dot(a, wg[...]), dot(a, wu[...])
    by_act = dot(by, wd[...], ((1,), (1,))).astype(BF).astype(F32)
    sig = jax.nn.sigmoid(gate)
    silu = gate * sig
    act = (silu * up).astype(BF)
    by_up = (by_act * silu).astype(BF)
    by_gate = (by_act * up * (sig + silu * (1.0 - sig))).astype(BF)
    at, byt = at_s[t], byt_s[t]
    new = (dot(at, by_gate), dot(at, by_up), dot(byt, act))

    @pl.when(t == 0)
    def _():
        for acc, term in zip((acc_g, acc_u, acc_d), new):
            acc[...] = term

    @pl.when(t > 0)
    def _():
        for acc, term in zip((acc_g, acc_u, acc_d), new):
            acc[...] += term

    if inner:
        term = dot(by_gate, wg[...], ((1,), (1,))) + dot(by_up, wu[...], ((1,), (1,)))

        @pl.when(j == 0)
        def _():
            by_a[here, :] = term

        @pl.when(j > 0)
        def _():
            by_a[here, :] += term

        @pl.when(j == chunks - 1)
        def _():
            g = by_a[here, :].astype(BF).astype(F32)
            wide, scale = norm(h_ref[...])
            inside = jnp.mean(g * wide, -1, keepdims=True)
            back = scale * g - (scale * scale * scale * inside) * wide
            by_out[...] = by_ref[...] + back.astype(BF)

    @pl.when(t == steps - 1)
    def _():
        for k, acc in enumerate((acc_g, acc_u)):
            for i in range(side):
                for n in range(side):
                    terms[k, i, n] = acc[pl.ds((i * side + n) * rows, rows), :].astype(BF)
        acc_d[...] = acc_d[...].T
        for i in range(side):
            for n in range(side):
                terms[2, i, n] = acc_d[pl.ds((i * side + n) * rows, rows), :].astype(BF)

    @pl.when((j == chunks - 1) & (t == steps - 1))
    def _():
        zero()
        one()
        two()
        three()
        four(chunks - 1)


def backward(side, h, by, weights, inner, number):
    tokens, d = h.shape
    ff = weights[0].shape[1]
    chunks, steps = ff // d, 8
    tile, rows = tokens // steps, d // side // side
    stream = pl.BlockSpec((tile, d), lambda j, t: (t, 0))
    out_shape = [jax.ShapeDtypeStruct((chunks, 3, rows, d), BF)]
    out_specs = [pl.BlockSpec((chunks, 3, rows, d), lambda j, t: (0, 0, 0, 0))]
    scratch = []
    if inner:
        out_shape.append(jax.ShapeDtypeStruct(h.shape, BF))
        out_specs.append(pl.BlockSpec((tile, d), lambda j, t: (jnp.where(j == chunks - 1, t, 0), 0)))
        scratch.append(pltpu.VMEM((tokens, d), F32))
    scratch += [pltpu.VMEM((tokens, d), BF), pltpu.VMEM((steps, d, tile), BF), pltpu.VMEM((steps, d, tile), BF)]
    scratch += [pltpu.VMEM((d, d), F32)] * 3 + [pltpu.VMEM((3, side, side, rows, d), BF)]
    scratch += scatter_scratch(side, rows, d) + [pltpu.SemaphoreType.DMA((24,)), pltpu.SemaphoreType.DMA((24,))]
    return pl.pallas_call(
        functools.partial(backward_kernel, side, chunks, steps, (0, 2, 5, 6, 7), inner),
        grid=(chunks, steps),
        out_shape=out_shape,
        in_specs=[stream, stream]
        + [pl.BlockSpec((d, d), lambda j, t: (0, j))] * 2
        + [pl.BlockSpec((d, d), lambda j, t: (j, 0))],
        out_specs=out_specs,
        scratch_shapes=scratch,
        compiler_params=pltpu.CompilerParams(
            collective_id=number, has_side_effects=True, vmem_limit_bytes=VMEM, dimension_semantics=("arbitrary", "arbitrary")
        ),
        cost_estimate=pl.CostEstimate(flops=(16 if inner else 12) * tokens * d * ff, bytes_accessed=30 * tokens * d, transcendentals=tokens * ff),
        name="backward",
    )(h, by, *weights)


def total_kernel(side, part_ref, out_ref, got, held, send, recv):
    x, y, near = place(side)
    greet_all = [x * side + (y + s) % side for s in range(1, side)], [(x + s) % side * side + y for s in range(1, side)]
    barrier = pltpu.get_barrier_semaphore()
    for peers in greet_all:
        for other in peers:
            pl.semaphore_signal(barrier, inc=1, device_id={"dp": other}, device_id_type=pl.DeviceIdType.MESH)
    pl.semaphore_wait(barrier, 2 * (side - 1))
    held[0] = part_ref[...]
    for phase, peers in enumerate(greet_all):
        sent = [remote(held.at[phase], got.at[phase, s], (send.at[phase], recv.at[phase]), s, other) for s, other in enumerate(peers)]
        for c in sent:
            c.start()
        for c in sent:
            c.wait()
        sum_ = held[phase]
        for s in range(side - 1):
            sum_ = sum_ + got[phase, s]
        if phase == 0:
            held[1] = sum_
        else:
            out_ref[...] = sum_


def total(side, part):
    tile = (8, LANES)
    n = side - 1
    out = pl.pallas_call(
        functools.partial(total_kernel, side),
        out_shape=jax.ShapeDtypeStruct(tile, F32),
        in_specs=[pl.BlockSpec(memory_space=pltpu.VMEM)],
        out_specs=pl.BlockSpec(memory_space=pltpu.VMEM),
        scratch_shapes=[
            pltpu.VMEM((2, n) + tile, F32),
            pltpu.VMEM((2,) + tile, F32),
            pltpu.SemaphoreType.DMA((2, n)),
            pltpu.SemaphoreType.DMA((2, n)),
        ],
        compiler_params=pltpu.CompilerParams(collective_id=4, has_side_effects=True),
        name="total",
    )(jnp.broadcast_to(part, tile))
    return out[0, 0]


def adamw(w, m, v, g):
    m = 0.9 * m + 0.1 * g
    v = 0.95 * v + 0.05 * g * g
    step = m * lax.rsqrt(v + 1e-8) + 0.1 * w
    return (w - 0.02 * step).astype(BF), m, v


def solution(mesh):
    group = mesh.shape["dp"]
    side = math.isqrt(group)

    def step(x, dy, *arrays):
        weights, m, v = (arrays[i : i + 3] for i in (0, 3, 6))
        gate, up, down = weights
        layers, rows, ff = gate.shape
        d = rows * group
        chunks = ff // d
        spread = (layers, rows, group, chunks, rows)
        gate, up = (w.reshape(spread).swapaxes(2, 3).reshape(w.shape) for w in (gate, up))
        down = down.reshape(layers, chunks, rows, d)
        shards = [(gate[n], up[n], down[n]) for n in range(layers)]
        h, by = x[0], dy[0]
        kept = []
        whole = [flat(gather(side, shards[0]))]
        for number in range(layers - 1):
            kept.append(h)
            h, following = forward(side, h, whole[number], shards[number + 1])
            whole.append(flat(following))
        kept.append(h)
        mine = [None] * layers
        for number in reversed(range(layers)):
            out = backward(side, kept[number], by, whole[number], number > 0, 2 + min(number, 1))
            mine[number] = out[0]
            if number > 0:
                by = out[1]
        mine = jnp.stack(mine)
        squares = total(side, jnp.sum(mine.astype(F32) ** 2))
        count = group * mine.size
        factor = jnp.minimum(1.0, 0.5 * lax.rsqrt(squares / count + 1e-30))
        gradients = [mine[:, :, k].reshape(layers, chunks, rows, group, rows).transpose(0, 2, 3, 1, 4).reshape(layers, rows, ff) for k in range(2)]
        gradients.append(mine[:, :, 2].reshape(layers, chunks * rows, d))
        new = [adamw(w.astype(F32), m, v, g.astype(F32) * factor) for w, m, v, g in zip(weights, m, v, gradients, strict=True)]
        return tuple(one[which] for which in range(3) for one in new)

    states, cut = P(("rep", "dp"), None, None), P(None, "dp", None)
    return jax.shard_map(
        step,
        mesh=mesh,
        in_specs=(states, states) + (cut,) * 9,
        out_specs=(P("rep", "dp", None),) * 9,
        check_vma=False,
    )
```

time: 1000 us -> 747 us (0.75)
  Pallas kernels: 0 us -> 682 us
  matrix products: 528 us -> 0 us
  waiting for transfers between devices: 354 us -> 0 us
  blocking collectives: 39.7 us -> 0 us
  local copies, waits for them, and re-layouts: 25.7 us -> 44.3 us
  between operations: 17.7 us -> 1.93 us
  other arithmetic: 27.8 us -> 12.5 us
    pallas_call x0 -> x5, Pallas kernels: none -> 682 us  [the longest x2 491 us: backward(): pl.pallas_call(functools.partial(backward_kernel, side, chunks, steps, (0...]
    dot_general x15 -> x0, matrix products: 528 us -> none  [the longest x5 192 us: layer(): gate = jnp.dot(a, w['w_gate'], preferred_element_type=jnp.float32)]
    unnamed x12 -> x0, waiting for transfers between devices: 254 us -> none
    all_gather x6 -> x0, waiting for transfers between devices: 99 us -> none  [fetched(): lax.all_gather(w[number], 'dp', axis=0, tiled=True)]
    psum x1 -> x0, blocking collectives: 39.7 us -> none  [step(): squares = lax.psum(sum((jnp.sum(g * g) for g in gradients)), 'dp')]
    mul x0 -> x6, local copies, waits for them, and re-layouts: none -> 23.8 us  [step(): g.astype(F32) * factor]
    unnamed x31 -> x18, local copies, waits for them, and re-layouts: 17.8 us -> 0.04 us
    add_any x1 -> x0, other arithmetic: 11.8 us -> none  [normed(): wide = h.astype(jnp.float32)]
  transfers between devices with their start and end apart: 9 -> 0, of which waited for: 7 -> 0; matrix products, arithmetic and copies ran while one was open for 33% -> 0% of each run, Pallas kernels for 0% -> 0%
where the time goes in v1:
time: 747 us; the launch traced here: 740 us
  Pallas kernels  682 us (91%)
  local copies, waits for them, and re-layouts  44.3 us (6%)
  other arithmetic  12.5 us (2%)
    pallas_call x2, Pallas kernels, backward(): pl.pallas_call(functools.partial(backward_kernel, side, chunks, steps, (0...  491 us
    pallas_call x1, Pallas kernels, forward(): pl.pallas_call(functools.partial(forward_kernel, side, steps, (0, 3, 5, 1...  93.8 us
    pallas_call x1, Pallas kernels, gather(): pl.pallas_call(functools.partial(gather_kernel, side), out_shape=gathered...  85.6 us
    mul x6, local copies, waits for them, and re-layouts, step(): g.astype(F32) * factor  23.8 us

profile of v1, /device:TPU:96, one launch (start us, length us, event | category | flops | bytes accessed | tf_op | source)
XLA Modules:
  0.0 740.2 jit_solution(5565536063514911264)
XLA Ops:
  0.6 1.9 fusion.22
  2.5 3.4 reshape.81
  6.0 1.5 fusion.21
  7.5 0.0 copy-start
  7.5 0.1 copy.26
  7.7 0.0 copy-start.5
  7.7 1.6 squeeze.29.refs_4_
  9.3 0.0 copy-done
  9.3 0.1 copy.24
  9.4 1.6 squeeze.26.refs_0_
  11.0 0.0 copy-done.5
  11.0 2.5 reshape.82
  13.5 1.5 fusion.20
  15.1 0.0 copy-start.1
  15.1 0.1 copy.27
  15.2 1.6 squeeze.30.refs_5_
  16.8 0.0 copy-done.1
  16.8 0.1 copy.25
  17.0 1.6 squeeze.27.refs_1_
  18.5 85.6 %gather.1 = (bf16[4,4,40,3200]{3,2,1,0:T(8,128)(2,1)}, bf16[4,4,40,3200]{3,2,1,0:T(8,128)(2,1)}, bf16[5,4,4,40,640]{4,3,2,1,0:T(8,128)(2,1)}) custom-call(bf16[40,3200]{1,0:T(8,128)(2,1)} %squeeze.26.refs_0_, bf16[40,3200]{1,0:T(8,128)(2,1)} %squeeze.27.refs_1_, bf16[5,40,640]{2,1,0:T(8,128)(2,1)} %bitcast.48), custom_call_target="tpu_custom_call" | custom-call | tf_op jit(solution)/shard_map/gather/pallas_call | solution.py:135
  104.1 93.8 %forward.1 = (bf16[4096,640]{1,0:T(8,128)(2,1)}, bf16[4,4,40,3200]{3,2,1,0:T(8,128)(2,1)}, bf16[4,4,40,3200]{3,2,1,0:T(8,128)(2,1)}, bf16[5,4,4,40,640]{4,3,2,1,0:T(8,128)(2,1)}) custom-call(bf16[4096,640]{1,0:T(8,128)(2,1)} %bitcast.51, bf16[640,3200]{1,0:T(8,128)(2,1)} %bitcast.53, bf16[640,3200]{1,0:T(8,128)(2,1)} %bitcast.55, ...), custom_call_target="tpu_custom_call" | custom-call | flops 50331648000 | bytes 52428800 | tf_op jit(solution)/shard_map/forward/pallas_call | solution.py:188
  197.9 278.1 %backward.2 = (bf16[5,3,40,640]{3,2,1,0:T(8,128)(2,1)}, bf16[4096,640]{1,0:T(8,128)(2,1)}) custom-call(bf16[4096,640]{1,0:T(8,128)(2,1)} %get-tuple-element.21.refs_0_, bf16[4096,640]{1,0:T(8,128)(2,1)} %bitcast.50, bf16[640,3200]{1,0:T(8,128)(2,1)} %bitcast.59, bf16[640,3200]{1,0:T(8,128)(2,1)} %bitcast.60, bf16[3200,640]{1,0:T(8,128)(2,1)} %bitcast.61), custom_call_target="tpu_custom_call" | custom-call | flops 134217728000 | bytes 78643200 | tf_op jit(solution)/shard_map/backward/pallas_call | solution.py:419
  476.0 213.4 %backward.3 = bf16[5,3,40,640]{3,2,1,0:T(8,128)(2,1)} custom-call(bf16[4096,640]{1,0:T(8,128)(2,1)} %bitcast.52, bf16[4096,640]{1,0:T(8,128)(2,1)} %get-tuple-element.25.refs_1_, bf16[640,3200]{1,0:T(8,128)(2,1)} %bitcast.54, bf16[640,3200]{1,0:T(8,128)(2,1)} %bitcast.56, bf16[3200,640]{1,0:T(8,128)(2,1)} %bitcast.58), custom_call_target="tpu_custom_call" | custom-call | flops 100663296000 | bytes 78643200 | tf_op jit(solution)/shard_map/backward/pallas_call | solution.py:419
  689.4 2.8 multiply_reduce_fusion
  692.2 0.0 copy-start.3
  692.2 0.0 copy-start.7
  692.2 0.0 copy-start.8
  692.2 1.4 broadcast_in_dim.3.part_ref
  693.6 10.7 %total.1 = f32[8,128]{1,0:T(8,128)} custom-call(f32[8,128]{1,0:T(8,128)} %broadcast_in_dim.3.part_ref), custom_call_target="tpu_custom_call" | custom-call | tf_op jit(solution)/shard_map/total/pallas_call | solution.py:463
  704.3 1.2 slice.43
  706.1 3.0 convert_multiply_fusion.3
  709.1 0.0 copy-done.3
  709.1 0.0 copy-done.7
  709.1 0.0 copy-done.8
  709.1 1.8 fusion.8
  710.9 3.3 mul.122
  714.2 4.2 copy.33
  718.5 4.8 mul.124
  723.3 3.3 mul.134
  726.6 4.2 copy.32
  730.8 0.0 copy-start.2
  730.8 0.0 copy-start.4
  730.8 0.0 copy-start.6
  730.8 3.9 mul.136
  734.8 0.0 copy-done.2
  734.8 0.0 copy-done.4
  734.8 0.0 copy-done.6
  734.8 5.0 fusion.2
Async XLA Ops:
  7.5 1.8 copy-start
  7.7 3.4 copy-start.5
  15.1 1.8 copy-start.1
  692.2 17.0 %copy-start.3 = (bf16[2,200,640]{2,1,0:T(8,128)(2,1)S(1)}, bf16[2,200,640]{2,1,0:T(8,128)(2,1)}, u32[]{:S(2)}) copy-start(bf16[2,200,640]{2,1,0:T(8,128)(2,1)} %param.15) | copy-start | bytes 1536004
  692.2 17.0 %copy-start.7 = (f32[2,200,640]{2,1,0:T(8,128)S(1)}, f32[2,200,640]{2,1,0:T(8,128)}, u32[]{:S(2)}) copy-start(f32[2,200,640]{2,1,0:T(8,128)} %param.21) | copy-start | bytes 3072004
  692.2 17.0 %copy-start.8 = (f32[2,200,640]{2,1,0:T(8,128)S(1)}, f32[2,200,640]{2,1,0:T(8,128)}, u32[]{:S(2)}) copy-start(f32[2,200,640]{2,1,0:T(8,128)} %param.18) | copy-start | bytes 3072004
  730.8 3.9 copy-start.2
  730.8 3.9 copy-start.4
  730.8 3.9 copy-start.6
